TPU v7x, 32 devices: a whole 2x2x4 slice. The times are simulated.
32 devices in a mesh: fsdp: 4 (over y, x), tenant: 4 (over z), dp: 2 (over core).
Axes of the slice: x: 2, y: 2, z: 4, core: 2. Of those that a mesh axis runs over, the one named last changes fastest.
Arguments:
- tokens: bfloat16 [3072, 5120], P(('fsdp', 'dp'), 'tenant'), may hold values from -6 to 6
- block_tenant_index: int32 [48], P(('fsdp', 'dp')), may hold values from 0 to 7
- ranks: int32 [8], replicated, may hold values from 16 to 64, as said below
- frozen_up_weight: bfloat16 [5120, 14336], P(('fsdp', 'dp'), 'tenant'), may hold values from -0.078125 to 0.078125
- tenant_down_adapters: bfloat16 [8, 64, 5120], P('tenant'), may hold values from -0.078125 to 0.078125
- tenant_up_adapters: bfloat16 [8, 64, 14336], P('tenant'), may hold values from -0.75 to 0.75
- cotangent: bfloat16 [3072, 14336], P(('fsdp', 'dp'), 'tenant'), may hold values from -6 to 6
Outputs:
- hidden_out: bfloat16 [3072, 14336], P(('fsdp', 'dp'), 'tenant')
- grad_tokens: bfloat16 [3072, 5120], P(('fsdp', 'dp'), 'tenant')
- grad_down: float32 [8, 64, 5120], P('dp', None, 'tenant')
- grad_up: float32 [8, 64, 14336], P('dp', None, 'tenant')
Inputs may be any that keep to these rules, and one draw needn't show every extreme that they name: `ranks`: multiples of 16; some tenant has rank 64.
All inputs are finite; a program needn't handle non-finite values.
Results may differ from a plain program's by a relative error of at most 0.0034.
Values may be sent and summed in bfloat16 or wider, within the bound.
No kernel may reach another device: no remote copies, remote signals or barrier semaphores. Data moves between devices by JAX's collectives and lax.ppermute only.
A program may use at most 128 MiB of HBM per device.

v0:
```python
import jax
import jax.numpy as jnp
from jax import lax
from jax.sharding import PartitionSpec as P

BLOCK = 64
alpha_scale = 32.0


def make_gain(block_tenant_index, ranks, rows, largest_rank):
    tenants = ranks.shape[0]
    rows_tenant = jnp.repeat(block_tenant_index, BLOCK, total_repeat_length=rows)
    columns = jnp.arange(tenants * largest_rank, dtype=jnp.int32)
    col_tenant = columns // largest_rank
    col_slot = columns % largest_rank
    ranks_col = jnp.repeat(ranks, largest_rank, total_repeat_length=tenants * largest_rank)
    keep = (rows_tenant[:, None] == col_tenant[None, :]) & (col_slot[None, :] < ranks_col[None, :])
    scale_col = alpha_scale / ranks_col.astype(jnp.float32)
    return jnp.where(keep, scale_col[None, :], jnp.float32(0.0))


def shards(
    tokens,
    block_tenant_index,
    ranks,
    frozen_up_weight,
    tenant_down_adapters,
    tenant_up_adapters,
    cotangent,
):
    rows = tokens.shape[0]
    local_d = tokens.shape[1]
    local_f = cotangent.shape[1]
    tenants = ranks.shape[0]
    largest_rank = tenant_down_adapters.shape[1]
    gain = make_gain(block_tenant_index, ranks, rows, largest_rank)
    whole = lax.all_gather(tokens, "tenant", axis=1, tiled=True)
    weight = lax.all_gather(frozen_up_weight, ("fsdp", "dp"), axis=0, tiled=True)
    down_part, up_adapter_slice = (
        lax.all_to_all(tenant_down_adapters, "tenant", split_axis=2, concat_axis=0, tiled=True),
        lax.all_to_all(tenant_up_adapters, "tenant", split_axis=2, concat_axis=0, tiled=True),
    )
    local_down = down_part.reshape(tenants * largest_rank, local_d)
    partial_proj = lax.dot_general(
        tokens, local_down, (((1,), (1,)), ((), ())), preferred_element_type=jnp.float32
    )
    proj = lax.psum(partial_proj, "tenant")
    flattened_up = up_adapter_slice.reshape(tenants * largest_rank, local_f)
    adapted = (proj * gain).astype(jnp.bfloat16)
    base = jnp.dot(whole, weight, preferred_element_type=jnp.float32)
    hidden_out = (base + jnp.dot(adapted, flattened_up, preferred_element_type=jnp.float32)).astype(
        jnp.bfloat16
    )
    back_part = lax.dot_general(
        cotangent, flattened_up, (((1,), (1,)), ((), ())), preferred_element_type=jnp.float32
    )
    back = lax.psum(back_part, "tenant")
    adapted_grad = (back * gain).astype(jnp.bfloat16)
    base_back = lax.dot_general(
        cotangent, weight, (((1,), (1,)), ((), ())), preferred_element_type=jnp.float32
    )
    grad_base = lax.psum_scatter(base_back, "tenant", scatter_dimension=1, tiled=True)
    grad_tokens = (
        grad_base + jnp.dot(adapted_grad, local_down, preferred_element_type=jnp.float32)
    ).astype(jnp.bfloat16)
    up_term = lax.dot_general(
        adapted, cotangent, (((0,), (0,)), ((), ())), preferred_element_type=jnp.float32
    )
    down_term = lax.dot_general(
        adapted_grad, tokens, (((0,), (0,)), ((), ())), preferred_element_type=jnp.float32
    )
    up_term = up_term.reshape(tenants, largest_rank, local_f)
    down_term = down_term.reshape(tenants, largest_rank, local_d)
    down_share, up_share = (
        lax.psum_scatter(down_term, "dp", scatter_dimension=0, tiled=True),
        lax.psum_scatter(up_term, "dp", scatter_dimension=0, tiled=True),
    )
    grad_down, grad_up = lax.psum((down_share, up_share), "fsdp")
    return (hidden_out, grad_tokens, grad_down, grad_up)


def solution(mesh):
    return jax.shard_map(
        shards,
        mesh=mesh,
        in_specs=(
            P(("fsdp", "dp"), "tenant"),
            P(("fsdp", "dp")),
            P(),
            P(("fsdp", "dp"), "tenant"),
            P("tenant", None, None),
            P("tenant", None, None),
            P(("fsdp", "dp"), "tenant"),
        ),
        out_specs=(
            P(("fsdp", "dp"), "tenant"),
            P(("fsdp", "dp"), "tenant"),
            P("dp", None, "tenant"),
            P("dp", None, "tenant"),
        ),
        check_vma=False,
    )
```

profile of v0, /device:TPU:0, one launch (start us, length us, event | category | flops | bytes accessed | tf_op | source)
XLA Modules:
  0.0 692.7 jit_solution(15375952981959615952)
XLA Ops:
  8.0 6.4 copy.13
  14.5 4.7 reshape.322
  19.1 6.3 all-to-all-start
  25.5 15.8 %copy.16 = bf16[2,64,14336]{1,0,2:T(2,128)(2,1)} copy(bf16[2,64,14336]{2,1,0:T(8,128)(2,1)} %param.16) | data formatting | bytes 7340032 | tf_op args[5]
  41.3 8.6 %reshape.320 = bf16[4,2,229376]{2,1,0:T(2,128)(2,1)} reshape(bf16[14336,2,64]{2,1,0:T(2,128)(2,1)} %bitcast.77) | data formatting | bytes 7340032
  49.9 7.1 %all-to-all-done = bf16[4,2,81920]{2,1,0:T(2,128)(2,1)} async-done(((bf16[4,2,81920]{2,1,0:T(2,128)(2,1)}), bf16[4,2,81920]{2,1,0:T(2,128)(2,1)}, u32[]{:S(2)}, u32[]{:S(2)}) %all-to-all-start) | async-done | bytes 1310752 | tf_op jit(solution)/shard_map/all_to_all | solution.py:40
  56.9 4.8 all-to-all-start.1
  61.8 4.6 reshape.323
  66.4 7.4 %copy.19 = bf16[2,64,4,1280]{3,2,1,0:T(4,128)(2,1)} copy(bf16[2,64,4,1280]{1,0,3,2:T(2,128)(2,1)} %bitcast.82) | data formatting | bytes 2621440 | tf_op jit(solution)/shard_map/all_to_all | solution.py:40
  73.8 1.4 copy.15
  76.3 2.8 fusion.26
  79.1 64.2 %all-to-all-done.1 = bf16[4,2,229376]{2,1,0:T(2,128)(2,1)} async-done(((bf16[4,2,229376]{2,1,0:T(2,128)(2,1)}), bf16[4,2,229376]{2,1,0:T(2,128)(2,1)}, u32[]{:S(2)}, u32[]{:S(2)}) %all-to-all-start.1) | async-done | bytes 3670048 | tf_op jit(solution)/shard_map/all_to_all | solution.py:41
  143.3 8.4 %reshape.321 = bf16[14336,2,64]{2,1,0:T(2,128)(2,1)} reshape(bf16[4,2,229376]{2,1,0:T(2,128)(2,1)} %all-to-all-done.1) | data formatting | bytes 7340032
  151.7 18.7 %copy.20 = bf16[2,64,4,3584]{3,2,1,0:T(4,128)(2,1)} copy(bf16[2,64,4,3584]{1,0,3,2:T(2,128)(2,1)} %bitcast.76) | data formatting | bytes 7340032 | tf_op jit(solution)/shard_map/all_to_all | solution.py:41
  170.4 2.7 copy.18
  173.1 1.8 copy-done.2
  174.9 2.5 fusion.28
  179.7 3.8 fusion.16
  183.5 4.5 compare_select_fusion.2
  188.9 56.8 %all-reduce.5.cloned.1.call-done = (f32[384,512]{1,0:T(8,128)}, f32[384,512]{1,0:T(8,128)}) async-done(((f32[384,512]{1,0:T(8,128)}, f32[384,512]{1,0:T(8,128)}), (f32[384,512]{1,0:T(8,128)}, f32[384,512]{1,0:T(8,128)})) %all-reduce.5.cloned.1.call-update) | async-done | bytes 1572880 | tf_op jit(solution)/shard_map/psum | solution.py:47
  245.7 4.0 fusion.17
  249.8 7.1 %fusion.20 = f32[512,3584]{1,0:T(8,128)} fusion(bf16[384,3584]{1,0:T(8,128)(2,1)S(1)} %copy-done, f32[384,512]{1,0:T(8,128)S(1)} %copy-done.5, f32[512]{0:T(512)S(1)} %convert_divide_fusion, s32[512]{0:T(512)S(1)} %add_select_fusion, s32[384]{0:T(512)S(1)} %and_select_fusion, pred[512]{0:T(512)(128)(4,1)S(1)} %get-tuple-element.32), kind=kOutput, calls=%fused_computation.52 | convolution fusion | flops 1410269184 | bytes 10885120 | tf_op jit(solution)/shard_map/dot_general | solution.py:66
  257.7 96.2 %all-gather.5.cloned.1.call-done = bf16[5120,3584]{1,0:T(8,128)(2,1)} async-done(((bf16[640,3584]{1,0:T(8,128)(2,1)}), bf16[5120,3584]{1,0:T(8,128)(2,1)}) %all-gather.5.cloned.1.call-update) | async-done | bytes 36700176 | tf_op jit(solution)/shard_map/all_gather | solution.py:38
  353.9 22.1 %fusion.27 = f32[384,5120]{1,0:T(8,128)} fusion(bf16[384,3584]{1,0:T(8,128)(2,1)S(1)} %copy-done, bf16[5120,3584]{1,0:T(8,128)(2,1)} %all-gather.5.cloned.1.call-done), kind=kOutput, calls=%fused_computation.57 | convolution fusion | flops 14092861440 | bytes 47316992 | tf_op jit(solution)/shard_map/dot_general | solution.py:59
  376.6 139.9 %all-gather.3.cloned.1.call-done = bf16[384,5120]{1,0:T(8,128)(2,1)} async-done(((bf16[384,1280]{1,0:T(8,128)(2,1)}), bf16[384,5120]{1,0:T(8,128)(2,1)}) %all-gather.3.cloned.1.call-update) | async-done | bytes 3932176 | tf_op jit(solution)/shard_map/all_gather | solution.py:37
  516.5 23.5 %fusion.25 = f32[384,3584]{1,0:T(8,128)} fusion(bf16[384,5120]{1,0:T(8,128)(2,1)} %all-gather.3.cloned.1.call-done, bf16[5120,3584]{1,0:T(8,128)(2,1)} %all-gather.5.cloned.1.call-done), kind=kOutput, calls=%fused_computation.55 | convolution fusion | flops 14092861440 | bytes 46137344 | tf_op jit(solution)/shard_map/dot_general | solution.py:50
  540.0 7.0 %fusion = bf16[384,3584]{1,0:T(8,128)(2,1)} fusion(f32[384,3584]{1,0:T(8,128)} %fusion.25, bf16[512,3584]{1,0:T(8,128)(2,1)} %bitcast.79, f32[384,512]{1,0:T(8,128)S(1)} %copy-done.5, f32[512]{0:T(512)S(1)} %convert_divide_fusion, s32[512]{0:T(512)S(1)} %add_select_fusion, s32[384]{0:T(512)S(1)} %and_select_fusion, pred[512]{0:T(512)(128)(4,1)S(1)} %get-tuple-element.32), kind=kOutput, calls=%fused_computation.1 | convolution fusion | flops 1413021696 | bytes 12720128 | tf_op jit(solution)/shard_map/dot_general | solution.py:51
  547.0 10.7 %reduce-scatter.4.cloned.1.call-done = f32[384,1280]{1,0:T(8,128)} async-done(((f32[384,5120]{1,0:T(8,128)}), f32[384,1280]{1,0:T(8,128)}) %reduce-scatter.4.cloned.1.call-update) | async-done | bytes 1966096 | tf_op jit(solution)/shard_map/reduce_scatter | solution.py:62
  557.7 3.3 fusion.1
  561.0 117.8 %all-reduce.7.cloned.1.call-done = (f32[4,64,1280]{2,1,0:T(8,128)}, f32[4,64,3584]{2,1,0:T(8,128)}) async-done(((f32[4,64,1280]{2,1,0:T(8,128)}, f32[4,64,3584]{2,1,0:T(8,128)}), (f32[4,64,1280]{2,1,0:T(8,128)}, f32[4,64,3584]{2,1,0:T(8,128)})) %all-reduce.7.cloned.1.call-update) | async-done | bytes 4980752 | tf_op jit(solution)/shard_map/psum | solution.py:78
  678.8 2.6 copy.29
  681.4 4.1 copy.30
  (48 shorter events, 5.6 us)
Async XLA Ops:
  8.0 166.9 %copy-start = (bf16[384,3584]{1,0:T(8,128)(2,1)S(1)}, bf16[384,3584]{1,0:T(8,128)(2,1)}, u32[]{:S(2)}) copy-start(bf16[384,3584]{1,0:T(8,128)(2,1)} %param.17) | copy-start | bytes 8257540
  19.1 37.8 %all-to-all-start = ((bf16[4,2,81920]{2,1,0:T(2,128)(2,1)}), bf16[4,2,81920]{2,1,0:T(2,128)(2,1)}, u32[]{:S(2)}, u32[]{:S(2)}) async-start(bf16[4,2,81920]{2,1,0:T(2,128)(2,1)} %reshape.322), calls=%async_computation | async-start | bytes 2621440 | tf_op jit(solution)/shard_map/all_to_all | solution.py:40
  56.9 86.3 %all-to-all-start.1 = ((bf16[4,2,229376]{2,1,0:T(2,128)(2,1)}), bf16[4,2,229376]{2,1,0:T(2,128)(2,1)}, u32[]{:S(2)}, u32[]{:S(2)}) async-start(bf16[4,2,229376]{2,1,0:T(2,128)(2,1)} %reshape.320), calls=%async_computation.1 | async-start | bytes 7340032 | tf_op jit(solution)/shard_map/all_to_all | solution.py:41
  61.8 184.0 %all-reduce.5.cloned.1.call-start = ((), (), s32[]{:S(2)}) async-start(), calls=%async_computation.10 | async-start | bytes 3145728 | tf_op jit(solution)/shard_map/psum | solution.py:47
  75.3 1.1 copy-start.3
  173.1 1.8 copy-start.2
  177.4 0.7 copy-start.8
  177.4 1.4 copy-start.7
  177.4 2.1 copy-start.10
  177.4 2.2 copy-start.9
  177.5 176.5 %all-gather.5.cloned.1.call-start = ((), (), s32[]{:S(2)}) async-start(), calls=%async_computation.6 | async-start | bytes 41287680 | tf_op jit(solution)/shard_map/all_gather | solution.py:38
  178.0 198.0 %reduce-scatter.6.cloned.1.call-start = ((), (), s32[]{:S(2)}) async-start(), calls=%async_computation.8 | async-start | bytes 3932160 | tf_op jit(solution)/shard_map/reduce_scatter | solution.py:75
  245.7 4.1 copy-start.5
  249.7 126.4 %reduce-scatter.8.cloned.1.call-start = ((), (), s32[]{:S(2)}) async-start(), calls=%async_computation.9 | async-start | bytes 11010048 | tf_op jit(solution)/shard_map/reduce_scatter | solution.py:76
  256.9 259.6 %all-gather.3.cloned.1.call-start = ((), (), s32[]{:S(2)}) async-start(), calls=%async_computation.5 | async-start | bytes 4915200 | tf_op jit(solution)/shard_map/all_gather | solution.py:37
  257.5 300.2 %reduce-scatter.4.cloned.1.call-start = ((), (), s32[]{:S(2)}) async-start(), calls=%async_computation.7 | async-start | bytes 9830400 | tf_op jit(solution)/shard_map/reduce_scatter | solution.py:62
  376.0 302.8 %all-reduce.7.cloned.1.call-start = ((), (), s32[]{:S(2)}) async-start(), calls=%async_computation.11 | async-start | bytes 9961472 | tf_op jit(solution)/shard_map/psum | solution.py:78
  540.0 17.8 %copy-start.4 = (bf16[4,2,64,1280]{3,2,1,0:T(8,128)(2,1)S(1)}, bf16[4,2,64,1280]{3,2,1,0:T(8,128)(2,1)}, u32[]{:S(2)}) copy-start(bf16[4,2,64,1280]{3,2,1,0:T(8,128)(2,1)} %copy-done.3) | copy-start | bytes 3932164
  540.0 17.8 %copy-start.6 = (f32[384,512]{1,0:T(8,128)S(1)}, f32[384,512]{1,0:T(8,128)}, u32[]{:S(2)}) copy-start(f32[384,512]{1,0:T(8,128)} %get-tuple-element.29) | copy-start | bytes 2359300
  678.8 6.8 copy-start.1
Sparse Core Ops, SparseCore 0:
  177.6 68.0 all-reduce.4
  249.9 16.8 reduce-scatter.5
  269.1 17.2 reduce-scatter.7
  376.1 181.5 reduce-scatter.3
  561.2 117.5 all-reduce.6
Sparse Core Ops, SparseCore 1:
  179.9 174.0 all-gather.4
  355.4 161.1 all-gather.2
where the time goes:
time: 695 us; the launch traced here: 693 us
  waiting for transfers between devices  494 us (71%)
  local copies, waits for them, and re-layouts  89.8 us (13%)
  matrix products  72.2 us (10%)
  between operations  15.4 us (2%)
  starting transfers between devices  11.6 us (2%)
  other arithmetic  9.35 us (1%)
    all_gather x1, waiting for transfers between devices, shards(): whole = lax.all_gather(tokens, 'tenant', axis=1, tiled=True)  140 us
    psum x1, waiting for transfers between devices, shards(): grad_down, grad_up = lax.psum((down_share, up_share), 'fsdp')  118 us
    all_gather x1, waiting for transfers between devices, shards(): lax.all_gather(frozen_up_weight, ('fsdp', 'dp'), axis=0, tiled=True)  96.2 us
    all_to_all x1, waiting for transfers between devices, shards(): lax.all_to_all(tenant_up_adapters, 'tenant', split_axis=2, concat_axis=0,...  64.2 us
    unnamed x30, local copies, waits for them, and re-layouts  58.2 us
    psum x1, waiting for transfers between devices, shards(): proj = lax.psum(partial_proj, 'tenant')  56.8 us
    dot_general x1, matrix products, shards(): base = jnp.dot(whole, weight, preferred_element_type=jnp.float32)  23.5 us
    dot_general x1, matrix products, shards(): lax.dot_general(cotangent, weight, (((1,), (1,)), ((), ())), preferred_el...  22.1 us
  transfers between devices with their start and end apart: 9, of which 7 were waited for; matrix products, arithmetic and copies ran while one was open for 17% of the time, Pallas kernels for 0%

commit v1 on v0

--- a/solution.py
+++ b/solution.py
@@ -44,7 +44,7 @@
     partial_proj = lax.dot_general(
         tokens, local_down, (((1,), (1,)), ((), ())), preferred_element_type=jnp.float32
     )
-    proj = lax.psum(partial_proj, "tenant")
+    proj = jnp.sum(lax.all_gather(partial_proj, "tenant"), axis=0)
     flattened_up = up_adapter_slice.reshape(tenants * largest_rank, local_f)
     adapted = (proj * gain).astype(jnp.bfloat16)
     base = jnp.dot(whole, weight, preferred_element_type=jnp.float32)

time: 695 us -> 830 us (1.19)
  waiting for transfers between devices: 494 us -> 630 us
    reduce_scatter x1, waiting for transfers between devices: 10.7 us -> 106 us  [shards(): lax.psum_scatter(base_back, 'tenant', scatter_dimension=1, tiled=True)]
    all_gather x1, waiting for transfers between devices: 96.2 us -> 167 us  [shards(): lax.all_gather(frozen_up_weight, ('fsdp', 'dp'), axis=0, tiled=True)]
    all_gather x0 -> x1, waiting for transfers between devices: none -> 60.9 us  [shards(): proj = jnp.sum(lax.all_gather(partial_proj, 'tenant'), axis=0)]
    all_gather x1, waiting for transfers between devices: 140 us -> 79.1 us  [shards(): whole = lax.all_gather(tokens, 'tenant', axis=1, tiled=True)]
    psum x1, waiting for transfers between devices: 56.8 us -> 16.3 us  [shards(): back = lax.psum(back_part, 'tenant')]
    reduce_scatter x1, waiting for transfers between devices: 0.02 us -> 10.6 us  [shards(): lax.psum_scatter(up_term, 'dp', scatter_dimension=0, tiled=True)]
    unnamed x30 -> x28, local copies, waits for them, and re-layouts: 58.2 us -> 58.3 us
  transfers between devices with their start and end apart: 9 -> 10, of which waited for: 7 -> 8; matrix products, arithmetic and copies ran while one was open for 17% -> 17% of each run, Pallas kernels for 0% -> 0%
where the time goes in v1:
time: 830 us; the launch traced here: 828 us
  waiting for transfers between devices  630 us (76%)
  local copies, waits for them, and re-layouts  89.9 us (11%)
  matrix products  71.1 us (9%)
  between operations  14.3 us (2%)
  other arithmetic  11.7 us (1%)
  starting transfers between devices  11.1 us (1%)
    all_gather x1, waiting for transfers between devices, shards(): lax.all_gather(frozen_up_weight, ('fsdp', 'dp'), axis=0, tiled=True)  167 us
    psum x1, waiting for transfers between devices, shards(): grad_down, grad_up = lax.psum((down_share, up_share), 'fsdp')  117 us
    reduce_scatter x1, waiting for transfers between devices, shards(): lax.psum_scatter(base_back, 'tenant', scatter_dimension=1, tiled=True)  106 us
    all_gather x1, waiting for transfers between devices, shards(): whole = lax.all_gather(tokens, 'tenant', axis=1, tiled=True)  79.1 us
    all_to_all x1, waiting for transfers between devices, shards(): lax.all_to_all(tenant_up_adapters, 'tenant', split_axis=2, concat_axis=0,...  71.1 us
    all_gather x1, waiting for transfers between devices, shards(): proj = jnp.sum(lax.all_gather(partial_proj, 'tenant'), axis=0)  60.9 us
    unnamed x28, local copies, waits for them, and re-layouts  58.3 us
    dot_general x1, matrix products, shards(): base = jnp.dot(whole, weight, preferred_element_type=jnp.float32)  23.9 us
  transfers between devices with their start and end apart: 10, of which 8 were waited for; matrix products, arithmetic and copies ran while one was open for 17% of the time, Pallas kernels for 0%

profile of v1, /device:TPU:0, one launch (start us, length us, event | category | flops | bytes accessed | tf_op | source)
XLA Modules:
  0.0 827.9 jit_solution(12817699277916810195)
XLA Ops:
  7.2 15.9 %copy.16 = bf16[2,64,14336]{1,0,2:T(2,128)(2,1)} copy(bf16[2,64,14336]{2,1,0:T(8,128)(2,1)} %param.16) | data formatting | bytes 7340032 | tf_op args[5]
  23.1 8.6 %reshape.321 = bf16[4,2,229376]{2,1,0:T(2,128)(2,1)} reshape(bf16[14336,2,64]{2,1,0:T(2,128)(2,1)} %bitcast.78) | data formatting | bytes 7340032
  31.7 6.3 all-to-all-start.1
  38.1 6.3 copy.13
  44.4 4.7 reshape.323
  49.0 71.1 %all-to-all-done.1 = bf16[4,2,229376]{2,1,0:T(2,128)(2,1)} async-done(((bf16[4,2,229376]{2,1,0:T(2,128)(2,1)}), bf16[4,2,229376]{2,1,0:T(2,128)(2,1)}, u32[]{:S(2)}, u32[]{:S(2)}) %all-to-all-start.1) | async-done | bytes 3670048 | tf_op jit(solution)/shard_map/all_to_all | solution.py:41
  120.2 4.3 all-to-all-start
  124.5 8.4 %reshape.322 = bf16[14336,2,64]{2,1,0:T(2,128)(2,1)} reshape(bf16[4,2,229376]{2,1,0:T(2,128)(2,1)} %all-to-all-done.1) | data formatting | bytes 7340032
  133.0 18.7 %copy.20 = bf16[2,64,4,3584]{3,2,1,0:T(4,128)(2,1)} copy(bf16[2,64,4,3584]{1,0,3,2:T(2,128)(2,1)} %bitcast.77) | data formatting | bytes 7340032 | tf_op jit(solution)/shard_map/all_to_all | solution.py:41
  151.7 2.7 copy.18
  156.2 2.5 fusion.28
  158.8 4.6 reshape.324
  163.4 7.4 copy.19
  173.3 2.8 fusion.26
  178.6 4.0 fusion.16
  182.6 4.4 compare_select_fusion.2
  187.8 16.3 %all-reduce.4.cloned.1.call-done = f32[384,512]{1,0:T(8,128)} async-done(((f32[384,512]{1,0:T(8,128)}), f32[384,512]{1,0:T(8,128)}) %all-reduce.4.cloned.1.call-update) | async-done | bytes 786448 | tf_op jit(solution)/shard_map/psum | solution.py:57
  204.0 3.9 fusion.17
  208.0 60.9 %all-gather.9.cloned.1.call-done = f32[1536,512]{1,0:T(8,128)} async-done(((f32[384,512]{1,0:T(8,128)}), f32[1536,512]{1,0:T(8,128)}) %all-gather.9.cloned.1.call-update) | async-done | bytes 3145744 | tf_op jit(solution)/shard_map/all_gather | solution.py:47
  268.9 2.3 reduce_sum.9
  271.2 5.4 fusion.20
  277.5 167.1 %all-gather.7.cloned.1.call-done = bf16[5120,3584]{1,0:T(8,128)(2,1)} async-done(((bf16[640,3584]{1,0:T(8,128)(2,1)}), bf16[5120,3584]{1,0:T(8,128)(2,1)}) %all-gather.7.cloned.1.call-update) | async-done | bytes 36700176 | tf_op jit(solution)/shard_map/all_gather | solution.py:38
  444.6 22.1 %fusion.27 = f32[384,5120]{1,0:T(8,128)} fusion(bf16[384,3584]{1,0:T(8,128)(2,1)S(1)} %copy-done, bf16[5120,3584]{1,0:T(8,128)(2,1)} %all-gather.7.cloned.1.call-done), kind=kOutput, calls=%fused_computation.57 | convolution fusion | flops 14092861440 | bytes 47316992 | tf_op jit(solution)/shard_map/dot_general | solution.py:59
  466.8 10.6 %reduce-scatter.8.cloned.1.call-done = f32[4,64,3584]{2,1,0:T(8,128)} async-done(((f32[8,64,3584]{2,1,0:T(8,128)}), f32[4,64,3584]{2,1,0:T(8,128)}) %reduce-scatter.8.cloned.1.call-update) | async-done | bytes 3670032 | tf_op jit(solution)/shard_map/reduce_scatter | solution.py:76
  477.4 79.1 %all-gather.5.cloned.1.call-done = bf16[384,5120]{1,0:T(8,128)(2,1)} async-done(((bf16[384,1280]{1,0:T(8,128)(2,1)}), bf16[384,5120]{1,0:T(8,128)(2,1)}) %all-gather.5.cloned.1.call-update) | async-done | bytes 3932176 | tf_op jit(solution)/shard_map/all_gather | solution.py:37
  556.5 23.9 %fusion.25 = f32[384,3584]{1,0:T(8,128)} fusion(bf16[384,5120]{1,0:T(8,128)(2,1)} %all-gather.5.cloned.1.call-done, bf16[5120,3584]{1,0:T(8,128)(2,1)} %all-gather.7.cloned.1.call-done), kind=kOutput, calls=%fused_computation.55 | convolution fusion | flops 14092861440 | bytes 46137344 | tf_op jit(solution)/shard_map/dot_general | solution.py:50
  580.4 7.0 fusion
  587.5 106.2 %reduce-scatter.4.cloned.1.call-done = f32[384,1280]{1,0:T(8,128)} async-done(((f32[384,5120]{1,0:T(8,128)}), f32[384,1280]{1,0:T(8,128)}) %reduce-scatter.4.cloned.1.call-update) | async-done | bytes 1966096 | tf_op jit(solution)/shard_map/reduce_scatter | solution.py:62
  693.6 3.3 fusion.1
  696.9 117.4 %all-reduce.6.cloned.1.call-done = (f32[4,64,1280]{2,1,0:T(8,128)}, f32[4,64,3584]{2,1,0:T(8,128)}) async-done(((f32[4,64,1280]{2,1,0:T(8,128)}, f32[4,64,3584]{2,1,0:T(8,128)}), (f32[4,64,1280]{2,1,0:T(8,128)}, f32[4,64,3584]{2,1,0:T(8,128)})) %all-reduce.6.cloned.1.call-update) | async-done | bytes 4980752 | tf_op jit(solution)/shard_map/psum | solution.py:78
  814.3 2.6 copy.28
  817.0 4.1 copy.29
  (50 shorter events, 8.5 us)
Async XLA Ops:
  7.2 149.0 %copy-start = (bf16[384,3584]{1,0:T(8,128)(2,1)S(1)}, bf16[384,3584]{1,0:T(8,128)(2,1)}, u32[]{:S(2)}) copy-start(bf16[384,3584]{1,0:T(8,128)(2,1)} %param.17) | copy-start | bytes 8257540
  31.7 88.4 %all-to-all-start.1 = ((bf16[4,2,229376]{2,1,0:T(2,128)(2,1)}), bf16[4,2,229376]{2,1,0:T(2,128)(2,1)}, u32[]{:S(2)}, u32[]{:S(2)}) async-start(bf16[4,2,229376]{2,1,0:T(2,128)(2,1)} %reshape.321), calls=%async_computation.1 | async-start | bytes 7340032 | tf_op jit(solution)/shard_map/all_to_all | solution.py:41
  120.2 38.6 %all-to-all-start = ((bf16[4,2,81920]{2,1,0:T(2,128)(2,1)}), bf16[4,2,81920]{2,1,0:T(2,128)(2,1)}, u32[]{:S(2)}, u32[]{:S(2)}) async-start(bf16[4,2,81920]{2,1,0:T(2,128)(2,1)} %reshape.323), calls=%async_computation | async-start | bytes 2621440 | tf_op jit(solution)/shard_map/all_to_all | solution.py:40
  124.5 79.6 %all-reduce.4.cloned.1.call-start = ((), (), s32[]{:S(2)}) async-start(), calls=%async_computation.8 | async-start | bytes 1572864 | tf_op jit(solution)/shard_map/psum | solution.py:57
  154.3 1.8 copy-start.2
  158.7 110.2 %all-gather.9.cloned.1.call-start = ((), (), s32[]{:S(2)}) async-start(), calls=%async_computation.11 | async-start | bytes 3932160 | tf_op jit(solution)/shard_map/all_gather | solution.py:47
  172.3 1.1 copy-start.3
  173.3 3.7 copy-start.7
  173.3 4.4 copy-start.6
  173.3 5.1 copy-start.9
  173.3 5.2 copy-start.8
  176.2 268.4 %all-gather.7.cloned.1.call-start = ((), (), s32[]{:S(2)}) async-start(), calls=%async_computation.6 | async-start | bytes 41287680 | tf_op jit(solution)/shard_map/all_gather | solution.py:38
  176.9 289.8 %reduce-scatter.6.cloned.1.call-start = ((), (), s32[]{:S(2)}) async-start(), calls=%async_computation.9 | async-start | bytes 3932160 | tf_op jit(solution)/shard_map/reduce_scatter | solution.py:75
  208.0 269.3 %reduce-scatter.8.cloned.1.call-start = ((), (), s32[]{:S(2)}) async-start(), calls=%async_computation.10 | async-start | bytes 11010048 | tf_op jit(solution)/shard_map/reduce_scatter | solution.py:76
  276.7 279.8 %all-gather.5.cloned.1.call-start = ((), (), s32[]{:S(2)}) async-start(), calls=%async_computation.5 | async-start | bytes 4915200 | tf_op jit(solution)/shard_map/all_gather | solution.py:37
  277.3 416.3 %reduce-scatter.4.cloned.1.call-start = ((), (), s32[]{:S(2)}) async-start(), calls=%async_computation.7 | async-start | bytes 9830400 | tf_op jit(solution)/shard_map/reduce_scatter | solution.py:62
  466.7 347.7 %all-reduce.6.cloned.1.call-start = ((), (), s32[]{:S(2)}) async-start(), calls=%async_computation.12 | async-start | bytes 9961472 | tf_op jit(solution)/shard_map/psum | solution.py:78
  580.4 113.2 %copy-start.4 = (bf16[4,2,64,1280]{3,2,1,0:T(8,128)(2,1)S(1)}, bf16[4,2,64,1280]{3,2,1,0:T(8,128)(2,1)}, u32[]{:S(2)}) copy-start(bf16[4,2,64,1280]{3,2,1,0:T(8,128)(2,1)} %copy-done.3) | copy-start | bytes 3932164
  580.4 113.2 %copy-start.5 = (f32[384,512]{1,0:T(8,128)S(1)}, f32[384,512]{1,0:T(8,128)}, u32[]{:S(2)}) copy-start(f32[384,512]{1,0:T(8,128)} %all-reduce.4.cloned.1.call-done) | copy-start | bytes 2359300
  814.3 6.8 copy-start.1
Sparse Core Ops, SparseCore 0:
  158.8 45.1 all-reduce.3
  206.2 62.6 all-gather.8
  270.8 173.7 all-gather.6
  447.2 10.4 reduce-scatter.5
  459.9 17.4 reduce-scatter.7
  478.8 77.6 all-gather.4
  558.8 134.7 reduce-scatter.3
  697.2 117.0 all-reduce.5
